TPU v7x, 32 devices: a whole 2x2x4 slice. The times are simulated.
32 devices in a mesh: groups: 2 (over y), tile: 4 (over z), tracer: 4 (over x, core).
Axes of the slice: x: 2, y: 2, z: 4, core: 2. Of those that a mesh axis runs over, the one named last changes fastest.
Arguments:
- species_amounts: float32 [64, 32, 128, 128], P(('groups', 'tracer'), None, 'tile'), parts along dimension 0, may hold values from 0.2 to 2
- face_currents: float32 [2, 64, 128, 128], P(None, 'groups', 'tile'), parts along dimension 1, may hold values from -1 to 1
- thermal_anomaly: float32 [64, 128, 128], P(('groups', 'tracer'), 'tile'), parts along dimension 0, may hold values from -4 to 4
- layer_total_per_profile: int32 [256, 128], P(('groups', 'tile')), parts along dimension 0, may hold values from 0 to 32
- consumed_species: int32 [32], replicated, may hold values from 0 to 31, each once
- attenuation_factor: float32 [32], replicated, may hold values from 0.009375 to 0.09375
- intake_speedup: float32 [32], replicated, may hold values from 0.3 to 3
- incoming_sunshine: float32 [256, 128], P(('groups', 'tile')), parts along dimension 0, may hold values from 0.5 to 2
Outputs:
- tracers_out: float32 [64, 32, 128, 128], P('groups', 'tracer', 'tile'), parts along dimension 0
- velocity_out: float32 [2, 64, 128, 128], P(None, ('groups', 'tracer'), 'tile'), parts along dimension 1
- temperature_out: float32 [64, 128, 128], P(('groups', 'tracer'), 'tile'), parts along dimension 0
There are 2 independent parts, one for each index of `groups`. A program takes and returns all parts, laid end to end along the dimension named above; an argument that names none is the same for every part. Nothing has to cross between parts.
Inputs may be any that keep to these rules, and one draw needn't show every extreme that they name: Levels 0 to layer_total_per_profile - 1 of a column are sea, deeper levels are land; 0 marks a land column. `consumed_species`: A permutation of the 32 tracers.
All inputs are finite; a program needn't handle non-finite values.
Results may differ from a plain program's by a relative error of at most 0.0003.
Values sent between devices are 32-bit elements; how exact they have to be, the bound alone decides.
A program may use at most 64 MiB of HBM per device.

v0:
```python
import jax
import jax.numpy as jnp
from jax import lax
from jax.sharding import PartitionSpec as P

DEPTH_LAYERS = 32


sub_step = 0.45
step_duration = 0.2
gravity = 0.5
viscosity = 0.2
coriolis_base = 0.5
beta_plane = 0.5
spreading_coefficient = 0.2
water_clear = 0.05
column_optical = 3.0
warming_coefficient = 5.0
light_half = 0.3
nutrient_half = 0.5


def padded(block, sides, width):
    for axis, dim in sides:
        count = lax.axis_size(axis)
        forward = [(i, i + 1) for i in range(count - 1)]
        forward.append((count - 1, 0))
        backward = [(target, source) for source, target in forward]
        low = lax.ppermute(
            lax.slice_in_dim(block, block.shape[dim] - width, None, axis=dim), axis, forward
        )
        high = lax.ppermute(lax.slice_in_dim(block, 0, width, axis=dim), axis, backward)
        block = jnp.concatenate([low, block, high], axis=dim)
    return block


def prefix(part, axis, combine, identity):
    place = lax.axis_index(axis)
    gathered = lax.all_gather(part, axis)
    state = jnp.zeros_like(part) + jnp.asarray(identity, part.dtype)

    def one(hop, state):
        return combine(state, lax.dynamic_index_in_dim(gathered, hop, 0, False))

    return lax.fori_loop(0, place, one, state)


def shift_south(values):
    return jnp.concatenate([jnp.zeros_like(values[..., :1]), values[..., :-1]], axis=-1)


def shift_north(values, offset=1):
    return jnp.concatenate([values[..., offset:], jnp.zeros_like(values[..., :offset])], axis=-1)


def wet_levels(depth_ext, first_level, level_count):
    levels = first_level + jnp.arange(level_count, dtype=jnp.int32)
    return (levels[:, None, None] < depth_ext[None]).astype(jnp.float32)


def limiter(left_slope, right_slope):
    smaller = jnp.minimum(jnp.abs(left_slope), jnp.abs(right_slope))
    return jnp.where(left_slope * right_slope > 0.0, jnp.sign(left_slope) * smaller, 0.0)


def face_flux(behind, centre, forward, beyond, speed):
    positive = speed * (centre + 0.5 * limiter(centre - behind, forward - centre))
    negative = speed * (forward - 0.5 * limiter(forward - centre, beyond - forward))
    return jnp.where(speed > 0.0, positive, negative)


def face_speeds(velocity_with_halo_border, wet_ext):
    east_speed = velocity_with_halo_border[0][:, :-1] * wet_ext[:, :-1] * wet_ext[:, 1:]
    north_speed = velocity_with_halo_border[1] * wet_ext * shift_north(wet_ext)
    return (east_speed, north_speed)


def flux_substep(extended, east_speed, north_speed):
    length = extended.shape[2]
    east_flux = face_flux(
        extended[:, :, 0 : length - 3],
        extended[:, :, 1 : length - 2],
        extended[:, :, 2 : length - 1],
        extended[:, :, 3:length],
        east_speed[:, 1 : length - 2],
    )
    middle = extended[:, :, 2 : length - 2]
    north_flux = face_flux(
        shift_south(middle),
        middle,
        shift_north(middle),
        shift_north(middle, 2),
        north_speed[:, 2 : length - 2],
    )
    spread = east_flux[:, :, 1:] - east_flux[:, :, :-1] + (north_flux - shift_south(north_flux))
    return middle - sub_step * spread


def advect(values, velocity_with_halo_border, wet_ext):
    east_speed, north_speed = face_speeds(velocity_with_halo_border, wet_ext)
    for repeat in range(2):
        extended = padded(values, (("tile", 2),), 2)
        values = flux_substep(extended, east_speed, north_speed)
    return values


def to_cells(values):
    return lax.all_to_all(values, "tracer", split_axis=1, concat_axis=0, tiled=True)


def laplacian(values):
    inner = values[:, 1:-1]
    return values[:, 2:] + values[:, :-2] + shift_north(inner) + shift_south(inner) - 4.0 * inner


def velocity_advance(flow_one, marine_mask_profile, thermal_profile_alone):
    east_vel = flow_one[0]
    north_vel = flow_one[1]
    ocean_profiles = east_vel.shape[1] - 2
    coriolis_y = (
        coriolis_base
        + beta_plane * jnp.arange(east_vel.shape[2], dtype=jnp.float32) / east_vel.shape[2]
    )
    centre_u = east_vel[:, 1 : ocean_profiles + 1]
    centre_v = north_vel[:, 1 : ocean_profiles + 1]
    v_bar = 0.25 * (
        centre_v + north_vel[:, 2:] + shift_south(centre_v) + shift_south(north_vel[:, 2:])
    )
    u_bar = 0.25 * (
        centre_u + east_vel[:, :-2] + shift_north(centre_u) + shift_north(east_vel[:, :-2])
    )
    marine_mask_interior = marine_mask_profile[:, 1 : ocean_profiles + 1]
    east_open = marine_mask_interior * marine_mask_profile[:, 2:]
    north_open = marine_mask_interior * shift_north(marine_mask_interior)
    heat_mid = thermal_profile_alone[:, 1 : ocean_profiles + 1]
    new_east = east_open * (
        centre_u
        + step_duration
        * (
            coriolis_y * v_bar
            - gravity * (thermal_profile_alone[:, 2:] - heat_mid)
            + viscosity * laplacian(east_vel)
        )
    )
    new_north = north_open * (
        centre_v
        + step_duration
        * (
            -coriolis_y * u_bar
            - gravity * (shift_north(heat_mid) - heat_mid)
            + viscosity * laplacian(north_vel)
        )
    )
    return (jnp.stack([new_east, new_north]), laplacian(thermal_profile_alone))


def optical_thickness(by_cells, attenuation_factor):
    summed = jnp.tensordot(
        attenuation_factor, jnp.abs(by_cells), axes=1, precision=lax.Precision.HIGHEST
    )
    return (water_clear + summed) * (column_optical / DEPTH_LAYERS)


def react(
    by_cells, optical, overhead, wet_mask, incoming_sunshine, intake_speedup, consumed_species
):
    depth_tau = overhead[None] + (jnp.cumsum(optical, axis=0) - optical)
    reaching = incoming_sunshine[None] * jnp.exp(-depth_tau)
    absorbed_part = 1.0 - jnp.exp(-optical)
    captured_radiance = reaching * absorbed_part * wet_mask
    mean_light = reaching * absorbed_part / optical
    light_limit = mean_light / (mean_light + light_half)
    pairing = (
        consumed_species[:, None] == jnp.arange(by_cells.shape[0], dtype=jnp.int32)[None]
    ).astype(jnp.float32)
    nutrient = jnp.tensordot(pairing, by_cells, axes=1, precision=lax.Precision.HIGHEST)
    uptake = (
        intake_speedup[:, None, None, None]
        * light_limit[None]
        * by_cells
        * nutrient
        / (nutrient_half + jnp.abs(nutrient))
    )
    consumed = jnp.tensordot(pairing.T, uptake, axes=1, precision=lax.Precision.HIGHEST)
    updated = by_cells + wet_mask[None] * (uptake - consumed)
    return (updated, captured_radiance)


def add_depths(earlier, later):
    return earlier + later


def on_device(
    species_amounts,
    face_currents,
    thermal_anomaly,
    layer_total_per_profile,
    consumed_species,
    attenuation_factor,
    intake_speedup,
    incoming_sunshine,
):
    layer_indices_here = thermal_anomaly.shape[0]
    ocean_profiles = thermal_anomaly.shape[1]
    first_level = lax.axis_index("tracer") * layer_indices_here
    margin = 2
    depth_ext = padded(layer_total_per_profile, (("tile", 0),), margin)
    flow_slice = lax.dynamic_slice_in_dim(face_currents, first_level, layer_indices_here, 1)
    velocity_with_halo_border = padded(flow_slice, (("tile", 2),), margin)
    wet_ext = wet_levels(depth_ext, first_level, layer_indices_here)
    by_cells = advect(to_cells(species_amounts), velocity_with_halo_border, wet_ext)
    thermal_profile_alone = padded(thermal_anomaly, (("tile", 1),), 1)
    flow_one = velocity_with_halo_border[:, :, margin - 1 : margin + ocean_profiles + 1]
    marine_mask_profile = wet_ext[:, margin - 1 : margin + ocean_profiles + 1]
    advanced_face_speeds, thermal_second_derivative = velocity_advance(
        flow_one, marine_mask_profile, thermal_profile_alone
    )
    marine_mask_interior = marine_mask_profile[:, 1:-1]
    optical = optical_thickness(by_cells, attenuation_factor)
    overhead = prefix(
        jnp.sum(optical, axis=0), "tracer", add_depths, jnp.zeros(optical.shape[1:], jnp.float32)
    )
    updated, captured_radiance = react(
        by_cells,
        optical,
        overhead,
        marine_mask_interior,
        incoming_sunshine,
        intake_speedup,
        consumed_species,
    )
    advanced_thermal_field = marine_mask_interior * (
        thermal_anomaly
        + step_duration * spreading_coefficient * thermal_second_derivative
        + warming_coefficient * captured_radiance
    )
    return (updated, advanced_face_speeds, advanced_thermal_field)


def solution(mesh):
    return jax.shard_map(
        on_device,
        mesh=mesh,
        in_specs=(
            P(("groups", "tracer"), None, "tile", None),
            P(None, "groups", "tile", None),
            P(("groups", "tracer"), "tile", None),
            P(("groups", "tile"), None),
            P(),
            P(),
            P(),
            P(("groups", "tile"), None),
        ),
        out_specs=(
            P("groups", "tracer", "tile", None),
            P(None, ("groups", "tracer"), "tile", None),
            P(("groups", "tracer"), "tile", None),
        ),
        check_vma=False,
    )
```

profile of v0, /device:TPU:0, one launch (start us, length us, event | category | flops | bytes accessed | tf_op | source)
XLA Modules:
  0.0 157.5 jit_solution(5242517074620127479)
XLA Ops:
  0.7 0.9 constant_dynamic-slice_fusion.1
  1.6 3.1 %collective-permute-start = (f32[2,8,2,128]{3,2,1,0:T(2,128)S(1)}, f32[2,8,2,128]{3,2,1,0:T(2,128)S(1)}, u32[]{:S(2)}, u32[]{:S(2)}) collective-permute-start(f32[2,8,2,128]{3,2,1,0:T(2,128)S(1)} %get-tuple-element.53), channel_id=1, source_target_pairs={{0,4},{4,8},{8,12},{12,0},{1,5},{5,9},{9,13},{13,1},{2,6},{6,10},{... | collective-permute-start | bytes 49160 | tf_op jit(solution)/shard_map/ppermute | solution.py:29
  4.7 2.1 %collective-permute-start.1 = (f32[2,8,2,128]{3,2,1,0:T(2,128)S(1)}, f32[2,8,2,128]{3,2,1,0:T(2,128)S(1)}, u32[]{:S(2)}, u32[]{:S(2)}) collective-permute-start(f32[2,8,2,128]{3,2,1,0:T(2,128)S(1)} %get-tuple-element.54), channel_id=1, source_target_pairs={{4,0},{8,4},{12,8},{0,12},{5,1},{9,5},{13,9},{1,13},{6,2},{10,6},{... | collective-permute-start | bytes 49160 | tf_op jit(solution)/shard_map/ppermute | solution.py:32
  6.7 0.7 fusion.83
  7.5 3.8 %collective-permute-start.3 = (s32[2,128]{1,0:T(2,128)S(1)}, s32[2,128]{1,0:T(2,128)S(1)}, u32[]{:S(2)}, u32[]{:S(2)}) collective-permute-start(s32[2,128]{1,0:T(2,128)S(1)} %get-tuple-element.77), channel_id=1, source_target_pairs={{4,0},{8,4},{12,8},{0,12},{5,1},{9,5},{13,9},{1,13},{6,2},{10,6},{... | collective-permute-start | bytes 3080 | tf_op jit(solution)/shard_map/ppermute | solution.py:32
  11.3 4.8 %copy.14 = f32[8,32,32,128]{3,2,0,1:T(8,128)} copy(f32[8,32,32,128]{3,2,1,0:T(8,128)} %param.10) | data formatting | bytes 8388608 | tf_op args[0]
  16.1 5.0 %all-to-all-start = ((f32[8,32,32,128]{3,2,0,1:T(8,128)}), f32[8,32,32,128]{3,2,0,1:T(8,128)}, u32[]{:S(2)}, u32[]{:S(2)}) async-start(f32[8,32,32,128]{3,2,0,1:T(8,128)} %copy.14), calls=%async_computation | async-start | bytes 8388608 | tf_op jit(solution)/shard_map/all_to_all | solution.py:108
  21.4 1.0 constant_dynamic-slice_fusion.2
  22.5 1.9 %collective-permute-start.9 = (f32[8,1,128]{2,1,0:T(1,128)S(1)}, f32[8,1,128]{2,1,0:T(1,128)S(1)}, u32[]{:S(2)}, u32[]{:S(2)}) collective-permute-start(f32[8,1,128]{2,1,0:T(1,128)S(1)} %get-tuple-element.72), channel_id=1, source_target_pairs={{0,4},{4,8},{8,12},{12,0},{1,5},{5,9},{9,13},{13,1},{2,6},{6,10},{... | collective-permute-start | bytes 12296 | tf_op jit(solution)/shard_map/ppermute | solution.py:29
  25.5 0.7 pad_maximum_fusion.5
  26.4 43.0 %all-to-all-done = f32[8,32,32,128]{3,2,0,1:T(8,128)} async-done(((f32[8,32,32,128]{3,2,0,1:T(8,128)}), f32[8,32,32,128]{3,2,0,1:T(8,128)}, u32[]{:S(2)}, u32[]{:S(2)}) %all-to-all-start) | async-done | bytes 4194336 | tf_op jit(solution)/shard_map/all_to_all | solution.py:108
  69.3 4.6 %copy.28 = f32[8,4,8,32,128]{4,0,1,3,2:T(8,128)S(1)} copy(f32[8,4,8,32,128]{4,3,0,2,1:T(8,128)} %bitcast.1) | data formatting | bytes 8388608 | tf_op jit(solution)/shard_map/all_to_all | solution.py:108
  73.9 1.6 %fusion.76 = (f32[32,8,32,127]{3,0,2,1:T(8,128)S(1)}, f32[32,8,32,127]{3,0,2,1:T(8,128)S(1)}) fusion(f32[32,8,32,128]{3,0,2,1:T(8,128)S(1)} %bitcast.45), kind=kLoop, calls=%fused_computation.133 | loop fusion | bytes 16646144 | tf_op jit(solution)/shard_map/slice | solution.py:49
  75.5 1.1 slice.293
  76.8 3.8 %collective-permute-start.5 = (f32[32,8,2,128]{3,0,2,1:T(8,128)S(1)}, f32[32,8,2,128]{3,0,2,1:T(8,128)S(1)}, u32[]{:S(2)}, u32[]{:S(2)}) collective-permute-start(f32[32,8,2,128]{3,0,2,1:T(8,128)S(1)} %get-tuple-element.52), channel_id=1, source_target_pairs={{4,0},{8,4},{12,8},{0,12},{5,1},{9,5},{13,9},{1,13},{6,2},{10,6},{... | collective-permute-start | bytes 786440 | tf_op jit(solution)/shard_map/ppermute | solution.py:32
  80.6 8.8 %multiply_select_fusion.3 = f32[32,8,32,128]{3,0,2,1:T(8,128)S(1)} fusion(f32[32,8,32,126]{3,0,2,1:T(8,128)S(1)} %slice.293, f32[32,8,32,127]{3,0,2,1:T(8,128)S(1)} %get-tuple-element.50, f32[32,8,32,127]{3,0,2,1:T(8,128)S(1)} %get-tuple-element.49, f32[8,32,128]{2,1,0:T(8,128)S(1)} %get-tuple-element.42, pred[8,32,128]{2,1,0:T(8,128)(4,1)S(1)} %get-tuple-element.41, ...), kind=kLoop, calls=%fused_computation.48 | loop fusion | flops 26214400 | bytes 21004288 | tf_op jit(solution)/shard_map/jit(_where)/select_n | solution.py:69
  89.4 1.0 collective-permute-done.5
  90.4 5.6 %multiply_select_fusion.1 = f32[32,8,33,128]{3,0,2,1:T(8,128)S(1)} fusion(f32[32,8,2,128]{3,0,2,1:T(8,128)S(1)} %collective-permute-done.5, f32[32,8,32,128]{3,0,2,1:T(8,128)S(1)} %bitcast.48, f32[32,8,2,128]{3,0,2,1:T(8,128)S(1)} %collective-permute-done.4, f32[8,33,128]{2,1,0:T(8,128)S(1)} %get-tuple-element.44, pred[8,33,128]{2,1,0:T(8,128)(4,1)S(1)} %get-tuple-element.43), kind=kLoop, calls=%fused_computation.26 | loop fusion | flops 31358976 | bytes 9212928 | tf_op jit(solution)/shard_map/jit(_where)/select_n | solution.py:69
  96.0 5.6 %fusion.17 = f32[32,8,32,128]{3,0,2,1:T(8,128)S(1)} fusion(f32[32,8,33,128]{3,0,2,1:T(8,128)S(1)} %multiply_select_fusion.1, f32[32,8,32,128]{3,0,2,1:T(8,128)S(1)} %multiply_select_fusion.3, f32[32,8,32,127]{3,0,2,1:T(8,128)S(1)} %bitcast.50, f32[8,4,8,32,128]{4,3,0,2,1:T(8,128)} %bitcast.1), kind=kLoop, calls=%fused_computation.38 | loop fusion | flops 5242880 | bytes 25133056 | tf_op jit(solution)/shard_map/sub | solution.py:96
  101.5 1.5 fusion.74
  103.0 1.1 slice.305
  104.3 3.8 %collective-permute-start.7 = (f32[32,8,2,128]{3,0,2,1:T(8,128)S(1)}, f32[32,8,2,128]{3,0,2,1:T(8,128)S(1)}, u32[]{:S(2)}, u32[]{:S(2)}) collective-permute-start(f32[32,8,2,128]{3,0,2,1:T(8,128)S(1)} %get-tuple-element.48), channel_id=1, source_target_pairs={{4,0},{8,4},{12,8},{0,12},{5,1},{9,5},{13,9},{1,13},{6,2},{10,6},{... | collective-permute-start | bytes 786440 | tf_op jit(solution)/shard_map/ppermute | solution.py:32
  108.1 7.5 %multiply_select_fusion.2 = f32[32,8,32,128]{3,0,2,1:T(8,128)} fusion(f32[32,8,32,126]{3,0,2,1:T(8,128)S(1)} %slice.305, f32[32,8,32,128]{3,0,2,1:T(8,128)S(1)} %fusion.17, f32[32,8,32,127]{3,0,2,1:T(8,128)S(1)} %get-tuple-element.46, f32[32,8,32,127]{3,0,2,1:T(8,128)S(1)} %get-tuple-element.45, f32[8,32,128]{2,1,0:T(8,128)S(1)} %get-tuple-element.42, ...), kind=kLoop, calls=%fused_computation.44 | loop fusion | flops 26214400 | bytes 21004288 | tf_op jit(solution)/shard_map/jit(_where)/select_n | solution.py:69
  115.6 1.9 %collective-permute-done.7 = f32[32,8,2,128]{3,0,2,1:T(8,128)S(1)} collective-permute-done((f32[32,8,2,128]{3,0,2,1:T(8,128)S(1)}, f32[32,8,2,128]{3,0,2,1:T(8,128)S(1)}, u32[]{:S(2)}, u32[]{:S(2)}) %collective-permute-start.7) | collective-permute-done | bytes 262176 | tf_op jit(solution)/shard_map/ppermute | solution.py:32
  117.6 6.5 %multiply_select_fusion = f32[32,8,33,128]{3,0,2,1:T(8,128)} fusion(f32[32,8,2,128]{3,0,2,1:T(8,128)S(1)} %collective-permute-done.7, f32[32,8,32,128]{3,0,2,1:T(8,128)S(1)} %fusion.17, f32[32,8,2,128]{3,0,2,1:T(8,128)S(1)} %collective-permute-done.6, f32[8,33,128]{2,1,0:T(8,128)S(1)} %get-tuple-element.44, pred[8,33,128]{2,1,0:T(8,128)(4,1)S(1)} %get-tuple-element.43), kind=kLoop, calls=%fused_computation.21 | loop fusion | flops 31358976 | bytes 9212928 | tf_op jit(solution)/shard_map/jit(_where)/select_n | solution.py:69
  124.1 9.9 %fusion.14 = f32[32,8,32,128]{3,0,2,1:T(8,128)} fusion(f32[32,8,32,128]{3,0,2,1:T(8,128)S(1)} %fusion.17, f32[32,8,33,128]{3,0,2,1:T(8,128)} %multiply_select_fusion, f32[32,8,32,128]{3,0,2,1:T(8,128)} %multiply_select_fusion.2, f32[32,8,32,127]{3,0,2,1:T(8,128)} %bitcast.49), kind=kLoop, calls=%fused_computation.34 | loop fusion | flops 5242880 | bytes 25133056 | tf_op jit(solution)/shard_map/sub | solution.py:96
  134.0 4.5 %fusion.18 = f32[1,8,32,128]{3,0,2,1:T(1,128)S(1)} fusion(f32[32,8,32,128]{3,0,2,1:T(8,128)} %fusion.14, f32[32]{0:T(128)S(1)} %copy-done), kind=kOutput, calls=%fused_computation.42 | convolution fusion | flops 13631488 | bytes 4325504 | tf_op jit(solution)/shard_map/dot_general | solution.py:158
  138.6 5.2 %all-gather = f32[128,128]{1,0:T(8,128)S(1)} all-gather(f32[32,128]{1,0:T(8,128)S(1)} %fusion.59), channel_id=2, replica_groups=mesh['groups'=2,'tile'=4,'tracer'=4] {'tracer'}, dimensions={0}, use_global_device_ids=true | all-gather | bytes 81920 | tf_op jit(solution)/shard_map/all_gather | solution.py:39
  143.9 4.1 %fusion.64 = f32[32,8,32,128]{3,0,2,1:T(8,128)S(1)} fusion(f32[32,8,32,128]{3,0,2,1:T(8,128)} %fusion.14, s32[32]{0:T(128)S(1)} %copy-done.5), kind=kOutput, calls=%fused_computation.116 | convolution fusion | flops 402654208 | bytes 8388736 | tf_op jit(solution)/shard_map/dot_general | solution.py:176
  148.1 0.8 fusion.37
  148.9 4.2 %multiply_add_fusion = f32[32,8,32,128]{3,0,2,1:T(8,128)S(1)} fusion(f32[32,8,32,128]{3,0,2,1:T(8,128)S(1)} %copy-done.1, f32[32,8,32,128]{3,0,2,1:T(8,128)S(1)} %fusion.64, f32[8,32,128]{2,1,0:T(8,128)S(1)} %get-tuple-element.69, f32[32]{0:T(128)S(1)} %copy-done.6, f32[8,32,128]{2,1,0:T(8,128)S(1)} %get-tuple-element.60, s32[32]{0:T(128)S(1)} %copy-done.5), kind=kOutput, calls=%fused_computation.40 | convolution fusion | flops 412091392 | bytes 12845312 | tf_op jit(solution)/shard_map/dot_general | solution.py:184
  153.1 4.4 %copy.17 = f32[32,8,32,128]{3,2,1,0:T(8,128)} copy(f32[32,8,32,128]{3,0,2,1:T(8,128)S(1)} %multiply_add_fusion) | data formatting | bytes 8388608
  (50 shorter events, 1.8 us)
Async XLA Ops:
  0.6 133.4 %copy-start = (f32[32]{0:T(128)S(1)}, f32[32]{0:T(128)}, u32[]{:S(2)}) copy-start(f32[32]{0:T(128)} %param.15) | copy-start | bytes 388
  1.6 23.2 %collective-permute-start = (f32[2,8,2,128]{3,2,1,0:T(2,128)S(1)}, f32[2,8,2,128]{3,2,1,0:T(2,128)S(1)}, u32[]{:S(2)}, u32[]{:S(2)}) collective-permute-start(f32[2,8,2,128]{3,2,1,0:T(2,128)S(1)} %get-tuple-element.53), channel_id=1, source_target_pairs={{0,4},{4,8},{8,12},{12,0},{1,5},{5,9},{9,13},{13,1},{2,6},{6,10},{... | collective-permute-start | bytes 49160 | tf_op jit(solution)/shard_map/ppermute | solution.py:29
  4.7 20.1 %collective-permute-start.1 = (f32[2,8,2,128]{3,2,1,0:T(2,128)S(1)}, f32[2,8,2,128]{3,2,1,0:T(2,128)S(1)}, u32[]{:S(2)}, u32[]{:S(2)}) collective-permute-start(f32[2,8,2,128]{3,2,1,0:T(2,128)S(1)} %get-tuple-element.54), channel_id=1, source_target_pairs={{4,0},{8,4},{12,8},{0,12},{5,1},{9,5},{13,9},{1,13},{6,2},{10,6},{... | collective-permute-start | bytes 49160 | tf_op jit(solution)/shard_map/ppermute | solution.py:32
  7.5 15.0 %collective-permute-start.2 = (s32[2,128]{1,0:T(2,128)S(1)}, s32[2,128]{1,0:T(2,128)S(1)}, u32[]{:S(2)}, u32[]{:S(2)}) collective-permute-start(s32[2,128]{1,0:T(2,128)S(1)} %get-tuple-element.76), channel_id=1, source_target_pairs={{0,4},{4,8},{8,12},{12,0},{1,5},{5,9},{9,13},{13,1},{2,6},{6,10},{... | collective-permute-start | bytes 3080 | tf_op jit(solution)/shard_map/ppermute | solution.py:29
  7.5 16.9 %collective-permute-start.3 = (s32[2,128]{1,0:T(2,128)S(1)}, s32[2,128]{1,0:T(2,128)S(1)}, u32[]{:S(2)}, u32[]{:S(2)}) collective-permute-start(s32[2,128]{1,0:T(2,128)S(1)} %get-tuple-element.77), channel_id=1, source_target_pairs={{4,0},{8,4},{12,8},{0,12},{5,1},{9,5},{13,9},{1,13},{6,2},{10,6},{... | collective-permute-start | bytes 3080 | tf_op jit(solution)/shard_map/ppermute | solution.py:32
  16.1 5.0 %copy-start.2 = (f32[8,32,128]{2,1,0:T(8,128)S(1)}, f32[8,32,128]{2,1,0:T(8,128)}, u32[]{:S(2)}) copy-start(f32[8,32,128]{2,1,0:T(8,128)} %param.12) | copy-start | bytes 393220
  16.1 8.3 %copy-start.3 = (s32[32,128]{1,0:T(8,128)S(1)}, s32[32,128]{1,0:T(8,128)}, u32[]{:S(2)}) copy-start(s32[32,128]{1,0:T(8,128)} %param.13) | copy-start | bytes 49156
  16.1 53.2 %all-to-all-start = ((f32[8,32,32,128]{3,2,0,1:T(8,128)}), f32[8,32,32,128]{3,2,0,1:T(8,128)}, u32[]{:S(2)}, u32[]{:S(2)}) async-start(f32[8,32,32,128]{3,2,0,1:T(8,128)} %copy.14), calls=%async_computation | async-start | bytes 8388608 | tf_op jit(solution)/shard_map/all_to_all | solution.py:108
  21.1 4.1 %collective-permute-start.8 = (f32[8,1,128]{2,1,0:T(1,128)S(1)}, f32[8,1,128]{2,1,0:T(1,128)S(1)}, u32[]{:S(2)}, u32[]{:S(2)}) collective-permute-start(f32[8,1,128]{2,1,0:T(1,128)S(1)} %get-tuple-element.73), channel_id=1, source_target_pairs={{4,0},{8,4},{12,8},{0,12},{5,1},{9,5},{13,9},{1,13},{6,2},{10,6},{... | collective-permute-start | bytes 12296 | tf_op jit(solution)/shard_map/ppermute | solution.py:32
  22.5 125.6 %collective-permute-start.9 = (f32[8,1,128]{2,1,0:T(1,128)S(1)}, f32[8,1,128]{2,1,0:T(1,128)S(1)}, u32[]{:S(2)}, u32[]{:S(2)}) collective-permute-start(f32[8,1,128]{2,1,0:T(1,128)S(1)} %get-tuple-element.72), channel_id=1, source_target_pairs={{0,4},{4,8},{8,12},{12,0},{1,5},{5,9},{9,13},{13,1},{2,6},{6,10},{... | collective-permute-start | bytes 12296 | tf_op jit(solution)/shard_map/ppermute | solution.py:29
  76.7 12.6 %collective-permute-start.4 = (f32[32,8,2,128]{3,0,2,1:T(8,128)S(1)}, f32[32,8,2,128]{3,0,2,1:T(8,128)S(1)}, u32[]{:S(2)}, u32[]{:S(2)}) collective-permute-start(f32[32,8,2,128]{3,0,2,1:T(8,128)S(1)} %get-tuple-element.51), channel_id=1, source_target_pairs={{0,4},{4,8},{8,12},{12,0},{1,5},{5,9},{9,13},{13,1},{2,6},{6,10},{... | collective-permute-start | bytes 786440 | tf_op jit(solution)/shard_map/ppermute | solution.py:29
  76.8 13.6 %collective-permute-start.5 = (f32[32,8,2,128]{3,0,2,1:T(8,128)S(1)}, f32[32,8,2,128]{3,0,2,1:T(8,128)S(1)}, u32[]{:S(2)}, u32[]{:S(2)}) collective-permute-start(f32[32,8,2,128]{3,0,2,1:T(8,128)S(1)} %get-tuple-element.52), channel_id=1, source_target_pairs={{4,0},{8,4},{12,8},{0,12},{5,1},{9,5},{13,9},{1,13},{6,2},{10,6},{... | collective-permute-start | bytes 786440 | tf_op jit(solution)/shard_map/ppermute | solution.py:32
  104.2 11.4 %collective-permute-start.6 = (f32[32,8,2,128]{3,0,2,1:T(8,128)S(1)}, f32[32,8,2,128]{3,0,2,1:T(8,128)S(1)}, u32[]{:S(2)}, u32[]{:S(2)}) collective-permute-start(f32[32,8,2,128]{3,0,2,1:T(8,128)S(1)} %get-tuple-element.47), channel_id=1, source_target_pairs={{0,4},{4,8},{8,12},{12,0},{1,5},{5,9},{9,13},{13,1},{2,6},{6,10},{... | collective-permute-start | bytes 786440 | tf_op jit(solution)/shard_map/ppermute | solution.py:29
  104.3 13.2 %collective-permute-start.7 = (f32[32,8,2,128]{3,0,2,1:T(8,128)S(1)}, f32[32,8,2,128]{3,0,2,1:T(8,128)S(1)}, u32[]{:S(2)}, u32[]{:S(2)}) collective-permute-start(f32[32,8,2,128]{3,0,2,1:T(8,128)S(1)} %get-tuple-element.48), channel_id=1, source_target_pairs={{4,0},{8,4},{12,8},{0,12},{5,1},{9,5},{13,9},{1,13},{6,2},{10,6},{... | collective-permute-start | bytes 786440 | tf_op jit(solution)/shard_map/ppermute | solution.py:32
  134.0 9.8 %copy-start.5 = (s32[32]{0:T(128)S(1)}, s32[32]{0:T(128)}, u32[]{:S(2)}) copy-start(s32[32]{0:T(128)} %param.14) | copy-start | bytes 388
  143.9 4.1 %copy-start.4 = (f32[32,128]{1,0:T(8,128)S(1)}, f32[32,128]{1,0:T(8,128)}, u32[]{:S(2)}) copy-start(f32[32,128]{1,0:T(8,128)} %param.17) | copy-start | bytes 49156
  143.9 5.0 %copy-start.1 = (f32[32,8,32,128]{3,0,2,1:T(8,128)S(1)}, f32[32,8,32,128]{3,0,2,1:T(8,128)}, u32[]{:S(2)}) copy-start(f32[32,8,32,128]{3,0,2,1:T(8,128)} %fusion.14) | copy-start | bytes 12582916
  143.9 5.0 %copy-start.6 = (f32[32]{0:T(128)S(1)}, f32[32]{0:T(128)}, u32[]{:S(2)}) copy-start(f32[32]{0:T(128)} %param.16) | copy-start | bytes 388
where the time goes:
time: 158 us
  other arithmetic  46.2 us (29%)
  waiting for transfers between devices  45.9 us (29%)
  starting transfers between devices  23.9 us (15%)
  local copies, waits for them, and re-layouts  22.5 us (14%)
  matrix products  12.8 us (8%)
  blocking collectives  5.24 us (3%)
    all_to_all x1, waiting for transfers between devices, to_cells(): lax.all_to_all(values, 'tracer', split_axis=1, concat_axis=0, tiled=True)  43 us
    select_n x4, other arithmetic, face_flux(): return jnp.where(speed > 0.0, positive, negative)  28.3 us
    sub x2, other arithmetic, flux_substep(): return middle - sub_step * spread  15.5 us
    ppermute x5, starting transfers between devices, padded(): lax.ppermute(lax.slice_in_dim(block, 0, width, axis=dim), axis, backward)  13.7 us
    unnamed x16, local copies, waits for them, and re-layouts  9.32 us
    all_gather x1, blocking collectives, prefix(): gathered = lax.all_gather(part, axis)  5.24 us
    ppermute x5, starting transfers between devices, padded(): lax.ppermute(lax.slice_in_dim(block, block.shape[dim] - width, None, axis...  5.14 us
    all_to_all x1, starting transfers between devices, to_cells(): lax.all_to_all(values, 'tracer', split_axis=1, concat_axis=0, tiled=True)  4.99 us
  transfers between devices with their start and end apart: 11, of which 3 were waited for; matrix products, arithmetic and copies ran while one was open for 45% of the time, Pallas kernels for 0%

commit v1 on v0

v1 whole, which is shorter than its diff:
```python
import functools

import jax
import jax.numpy as jnp
from jax import lax
from jax.experimental import pallas as pl
from jax.experimental.pallas import tpu as pltpu
from jax.sharding import PartitionSpec as P

MESH = pl.DeviceIdType.MESH

sub_step = 0.45
step_duration = 0.2
gravity = 0.5
viscosity = 0.2
coriolis_base = 0.5
beta_plane = 0.5
spreading_coefficient = 0.2
water_clear = 0.05
column_optical = 3.0
warming_coefficient = 5.0
light_half = 0.3
nutrient_half = 0.5

PAD = 8
EDGE = 4


def lane_index(shape):
    return lax.broadcasted_iota(jnp.int32, shape, len(shape) - 1)


def east(x):
    return pltpu.roll(x, x.shape[0] - 1, 0)


def west(x):
    return pltpu.roll(x, 1, 0)


def north(x):
    return jnp.where(lane_index(x.shape) == x.shape[1] - 1, 0.0, pltpu.roll(x, x.shape[1] - 1, 1))


def south(x):
    return jnp.where(lane_index(x.shape) == 0, 0.0, pltpu.roll(x, 1, 1))


def minmod(a, b):
    return jnp.maximum(jnp.minimum(a, b), 0.0) + jnp.minimum(jnp.maximum(a, b), 0.0)


def laplacian(x):
    return east(x) + west(x) + north(x) + south(x) - 4.0 * x


def substep(c, es, ns, lane):
    last = c.shape[1] - 1
    d = east(c) - c
    half = 0.5 * minmod(west(d), d)
    flux = es * jnp.where(es > 0.0, c + half, east(c - half))
    spread = flux - west(flux)
    d = jnp.where(lane == last, 0.0, pltpu.roll(c, last, 1)) - c
    half = 0.5 * minmod(jnp.where(lane == 0, c, pltpu.roll(d, 1, 1)), d)
    flux = ns * jnp.where(ns > 0.0, c + half, pltpu.roll(c - half, last, 1))
    return c - (spread + (flux - pltpu.roll(flux, 1, 1)))


def transport_kernel(
    tiles, ranks, cores, q,
    sp, fc, th, dep, att,
    cells, over, vel, heat,
    ext, fext, hext, dext, adv, tot, pre,
    h_send, h_recv, f_send, f_recv, s_send, s_recv, d_send, d_recv, o_send, o_recv,
    l_sem, lf_sem, ls_sem, own_sem,
):
    nt, nl, rows, width = sp.shape
    per = nl // ranks
    nc = per // q
    chips = ranks // cores
    chunks = ranks * nc
    full = rows + 2 * PAD
    r = lax.axis_index("tracer")
    z = lax.axis_index("tile")
    a, b = r // cores, lax.rem(r, cores)
    up, down = lax.rem(z + 1, tiles), lax.rem(z + tiles - 1, tiles)

    def target(s):
        ka, kb = lax.rem(1 + s // cores, chips), cores - 1 - lax.rem(s, cores)
        return lax.rem(a + ka, chips) * cores + lax.rem(b + kb, cores)

    def source(s):
        ka, kb = lax.rem(1 + s // cores, chips), cores - 1 - lax.rem(s, cores)
        return lax.rem(a + chips - ka, chips) * cores + lax.rem(b + cores - kb, cores)

    def first_level(n):
        return target(n // nc) * per + lax.rem(n, nc) * q

    low_rows = pl.ds(0, EDGE)
    high_rows = pl.ds(rows - EDGE, EDGE)
    from_low = pl.ds(PAD - EDGE, EDGE)
    from_high = pl.ds(PAD + rows, EDGE)
    body = pl.ds(PAD, rows)

    def pair(src, dst, lead, send, recv, at):
        return (
            pltpu.make_async_remote_copy(
                src.at[lead + (high_rows,)], dst.at[lead + (from_low,)],
                send.at[at + (0,)], recv.at[at + (0,)],
                device_id={"tile": up}, device_id_type=MESH,
            ),
            pltpu.make_async_remote_copy(
                src.at[lead + (low_rows,)], dst.at[lead + (from_high,)],
                send.at[at + (1,)], recv.at[at + (1,)],
                device_id={"tile": down}, device_id_type=MESH,
            ),
        )

    def species_edges(n):
        lead = (slice(None), pl.ds(first_level(n), q))
        return pair(sp, ext, lead, h_send, h_recv, (n,))

    def current_edges(n):
        lead = (slice(None), pl.ds(first_level(n), q))
        return pair(fc, fext, lead, f_send, f_recv, (n,))

    def heat_edges():
        return pair(th, hext, (slice(None),), s_send, s_recv, (0,))

    def depth_edges():
        return pair(dep, dext, (), s_send, s_recv, (1,))

    def species_local(n):
        lev = pl.ds(first_level(n), q)
        return pltpu.make_async_copy(sp.at[:, lev], ext.at[:, lev, body], l_sem.at[n])

    def block_copy(n):
        s, c = n // nc, lax.rem(n, nc)
        return pltpu.make_async_remote_copy(
            adv.at[:, pl.ds(first_level(n), q)],
            cells.at[pl.ds(r * nt, nt), pl.ds(c * q, q)],
            d_send.at[n], d_recv.at[n],
            device_id={"tracer": target(s)}, device_id_type=MESH,
        )

    def block_arrival(n):
        s, c = n // nc, lax.rem(n, nc)
        return pltpu.make_async_remote_copy(
            adv.at[:, pl.ds(first_level(n), q)],
            cells.at[pl.ds(source(s) * nt, nt), pl.ds(c * q, q)],
            d_send.at[n], d_recv.at[n],
            device_id={"tracer": target(s)}, device_id_type=MESH,
        )

    def own_copy(n):
        c = lax.rem(n, nc)
        return pltpu.make_async_copy(
            adv.at[:, pl.ds(first_level(n), q)],
            cells.at[pl.ds(r * nt, nt), pl.ds(c * q, q)],
            own_sem.at[c],
        )

    def over_copy(s, place):
        return pltpu.make_async_remote_copy(
            pre.at[target(s)], over.at[place], o_send.at[s], o_recv.at[s],
            device_id={"tracer": target(s)}, device_id_type=MESH,
        )

    fc_local = pltpu.make_async_copy(fc, fext.at[:, :, body], lf_sem.at[0])
    dep_local = pltpu.make_async_copy(dep, dext.at[body], lf_sem.at[1])
    th_local = pltpu.make_async_copy(th, hext.at[:, body], lf_sem.at[2])
    dep_local.start()
    fc_local.start()

    def start_local(n, carry):
        species_local(n).start()
        return carry

    lax.fori_loop(0, chunks, start_local, 0)
    th_local.start()

    barrier = pltpu.get_barrier_semaphore()
    for place in (up, down):
        pl.semaphore_signal(barrier, inc=1, device_id={"tile": place}, device_id_type=MESH)
    for s in range(ranks - 1):
        pl.semaphore_signal(barrier, inc=1, device_id={"tracer": target(s)}, device_id_type=MESH)
    pl.semaphore_wait(barrier, 2 + ranks - 1)

    for copy in depth_edges():
        copy.start()

    def start_edges(n, carry):
        for copy in current_edges(n) + species_edges(n):
            copy.start()
        return carry

    lax.fori_loop(0, chunks, start_edges, 0)
    for copy in heat_edges():
        copy.start()

    tot[...] = jnp.zeros_like(tot)
    dep_local.wait()
    fc_local.wait()
    for copy in depth_edges():
        copy.wait()
    lane = lane_index((full, width))

    def advance(n):
        species_local(n).wait()
        for copy in current_edges(n) + species_edges(n):
            copy.wait_recv()
        block = target(n // nc)
        level_0 = first_level(n)

        def one_level(i, carry):
            lev = level_0 + i
            wet = jnp.where(lev < dext[...], 1.0, 0.0)
            es = sub_step * (fext[0, lev] * wet * east(wet))
            ns = sub_step * (fext[1, lev] * wet * north(wet))

            def one_tracer(t, acc):
                c = substep(ext[t, lev], es, ns, lane)
                c = substep(c, es, ns, lane)[PAD:PAD + rows]
                adv[t, lev] = c
                return acc + att[r * nt + t] * jnp.abs(c)

            tot[block] = lax.fori_loop(0, nt, one_tracer, tot[block])
            return carry

        lax.fori_loop(0, q, one_level, 0)

    def advance_send(n, carry):
        advance(n)
        block_copy(n).start()
        return carry

    def advance_keep(n, carry):
        advance(n)
        own_copy(n).start()
        return carry

    lax.fori_loop(0, chunks - nc, advance_send, 0)
    lax.fori_loop(chunks - nc, chunks, advance_keep, 0)

    above = jnp.zeros((rows, width), jnp.float32)
    for place in range(ranks):
        pre[place] = above
        above = above + tot[place]
    own_over = pltpu.make_async_copy(pre.at[r], over.at[r], lf_sem.at[3])
    for s in range(ranks - 1):
        over_copy(s, r).start()
    own_over.start()

    th_local.wait()
    for copy in heat_edges():
        copy.wait()
    coriolis = coriolis_base + beta_plane * lane.astype(jnp.float32) / width

    def momentum(i, carry):
        lev = r * per + i
        u, v, heat_ext = fext[0, lev], fext[1, lev], hext[i]
        wet = jnp.where(lev < dext[...], 1.0, 0.0)
        v_east, u_west = east(v), west(u)
        v_bar = 0.25 * (v + v_east + south(v) + south(v_east))
        u_bar = 0.25 * (u + u_west + north(u) + north(u_west))
        new_u = u + step_duration * (
            coriolis * v_bar - gravity * (east(heat_ext) - heat_ext) + viscosity * laplacian(u)
        )
        new_v = v + step_duration * (
            -coriolis * u_bar - gravity * (north(heat_ext) - heat_ext) + viscosity * laplacian(v)
        )
        vel[0, i] = (wet * east(wet) * new_u)[PAD:PAD + rows]
        vel[1, i] = (wet * north(wet) * new_v)[PAD:PAD + rows]
        warmer = heat_ext + step_duration * spreading_coefficient * laplacian(heat_ext)
        heat[i] = warmer[PAD:PAD + rows]
        return carry

    lax.fori_loop(0, per, momentum, 0)

    def drain_edges(n, carry):
        for copy in current_edges(n) + species_edges(n):
            copy.wait_send()
        return carry

    lax.fori_loop(0, chunks, drain_edges, 0)

    def drain_own(n, carry):
        own_copy(n).wait()
        return carry

    lax.fori_loop(chunks - nc, chunks, drain_own, 0)
    own_over.wait()

    def drain_blocks(n, carry):
        block_arrival(n).wait_recv()
        block_copy(n).wait_send()
        return carry

    lax.fori_loop(0, chunks - nc, drain_blocks, 0)
    for s in range(ranks - 1):
        over_copy(s, source(s)).wait_recv()
        over_copy(s, r).wait_send()


def react_kernel(
    levels, per,
    cells, over, vel, heat, dep, sun, eaten, att, rate,
    out, vel_out, temp_out,
    sat, depth_tau, eater,
):
    step = pl.program_id(0)
    r = lax.axis_index("tracer")
    count = cells.shape[0]
    scale = column_optical / levels

    @pl.when(step == 0)
    def _():
        above = over[0]
        for place in range(1, over.shape[0]):
            above = above + over[place]
        clear = (r * per).astype(jnp.float32) * water_clear
        depth_tau[...] = (above + clear) * scale
        for t in range(count):
            eater[eaten[t]] = t

    vel_out[...] = vel[...]
    total = jnp.full(dep.shape, water_clear, jnp.float32)
    for t in range(count):
        x = cells[t, 0]
        size = jnp.abs(x)
        total = total + att[t] * size
        sat[t] = x / (nutrient_half + size)
    optical = total * scale
    tau = depth_tau[...]
    depth_tau[...] = tau + optical
    wet = jnp.where(r * per + step < dep[...], 1.0, 0.0)
    caught = sun[...] * jnp.exp(-tau) * (1.0 - jnp.exp(-optical))
    mean_light = caught / optical
    gain = wet * (mean_light / (mean_light + light_half))
    temp_out[0] = wet * (heat[0] + warming_coefficient * (caught * wet))
    for t in range(count):
        food, by = eaten[t], eater[t]
        x = cells[t, 0]
        change = rate[t] * (x * sat[food]) - rate[by] * (cells[by, 0] * sat[t])
        out[t, 0] = x + gain * change


def solution(mesh):
    tiles, ranks = mesh.shape["tile"], mesh.shape["tracer"]
    cores = 2 if ranks % 2 == 0 else 1

    def on_device(
        species_amounts,
        face_currents,
        thermal_anomaly,
        layer_total_per_profile,
        consumed_species,
        attenuation_factor,
        intake_speedup,
        incoming_sunshine,
    ):
        nt, nl, rows, width = species_amounts.shape
        per = nl // ranks
        q = 2 if per % 2 == 0 else 1
        chunks = nl // q
        full = rows + 2 * PAD
        f32 = jnp.float32
        any_space = pl.BlockSpec(memory_space=pl.ANY)
        vmem = pl.BlockSpec(memory_space=pltpu.VMEM)
        smem = pl.BlockSpec(memory_space=pltpu.SMEM)
        dma = pltpu.SemaphoreType.DMA
        cells, over, vel, heat = pl.pallas_call(
            functools.partial(transport_kernel, tiles, ranks, cores, q),
            out_shape=(
                jax.ShapeDtypeStruct((ranks * nt, per, rows, width), f32),
                jax.ShapeDtypeStruct((ranks, rows, width), f32),
                jax.ShapeDtypeStruct((2, per, rows, width), f32),
                jax.ShapeDtypeStruct((per, rows, width), f32),
            ),
            in_specs=[any_space] * 4 + [smem],
            out_specs=(any_space, any_space, vmem, vmem),
            scratch_shapes=[
                pltpu.VMEM((nt, nl, full, width), f32),
                pltpu.VMEM((2, nl, full, width), f32),
                pltpu.VMEM((per, full, width), f32),
                pltpu.VMEM((full, width), jnp.int32),
                pltpu.VMEM((nt, nl, rows, width), f32),
                pltpu.VMEM((ranks, rows, width), f32),
                pltpu.VMEM((ranks, rows, width), f32),
                dma((chunks, 2)), dma((chunks, 2)),
                dma((chunks, 2)), dma((chunks, 2)),
                dma((2, 2)), dma((2, 2)),
                dma((chunks,)), dma((chunks,)),
                dma((ranks,)), dma((ranks,)),
                dma((chunks,)), dma((4,)), dma((1,)), dma((per // q,)),
            ],
            compiler_params=pltpu.CompilerParams(
                collective_id=0, has_side_effects=True, vmem_limit_bytes=32 * 2**20
            ),
            name="transport",
        )(
            species_amounts, face_currents, thermal_anomaly,
            layer_total_per_profile, attenuation_factor,
        )
        count = ranks * nt
        column = pl.BlockSpec((count, 1, rows, width), lambda i: (0, i, 0, 0))
        flow = pl.BlockSpec((2, 1, rows, width), lambda i: (0, i, 0, 0))
        sheet = pl.BlockSpec((1, rows, width), lambda i: (i, 0, 0))
        flat = pl.BlockSpec((rows, width), lambda i: (0, 0))
        return pl.pallas_call(
            functools.partial(react_kernel, nl, per),
            grid=(per,),
            out_shape=(
                jax.ShapeDtypeStruct((count, per, rows, width), f32),
                jax.ShapeDtypeStruct((2, per, rows, width), f32),
                jax.ShapeDtypeStruct((per, rows, width), f32),
            ),
            in_specs=[
                column,
                pl.BlockSpec((ranks, rows, width), lambda i: (0, 0, 0)),
                flow, sheet, flat, flat, smem, smem, smem,
            ],
            out_specs=(column, flow, sheet),
            scratch_shapes=[
                pltpu.VMEM((count, rows, width), f32),
                pltpu.VMEM((rows, width), f32),
                pltpu.SMEM((count,), jnp.int32),
            ],
            compiler_params=pltpu.CompilerParams(
                dimension_semantics=("arbitrary",), vmem_limit_bytes=16 * 2**20
            ),
            name="react",
        )(
            cells, over, vel, heat, layer_total_per_profile, incoming_sunshine,
            consumed_species, attenuation_factor, intake_speedup,
        )

    return jax.shard_map(
        on_device,
        mesh=mesh,
        in_specs=(
            P(("groups", "tracer"), None, "tile", None),
            P(None, "groups", "tile", None),
            P(("groups", "tracer"), "tile", None),
            P(("groups", "tile"), None),
            P(),
            P(),
            P(),
            P(("groups", "tile"), None),
        ),
        out_specs=(
            P("groups", "tracer", "tile", None),
            P(None, ("groups", "tracer"), "tile", None),
            P(("groups", "tracer"), "tile", None),
        ),
        check_vma=False,
    )
```

time: 158 us -> 177 us (1.12)
  Pallas kernels: 0 us -> 170 us
  other arithmetic: 46.2 us -> 0 us
  waiting for transfers between devices: 45.9 us -> 0 us
  starting transfers between devices: 23.9 us -> 0 us
  local copies, waits for them, and re-layouts: 22.5 us -> 5.69 us
  matrix products: 12.8 us -> 0 us
  blocking collectives: 5.24 us -> 0 us
    pallas_call x0 -> x2, Pallas kernels: none -> 170 us  [the longest x1 165 us: on_device(): pl.pallas_call(functools.partial(transport_kernel, tiles, ranks, cores, q...]
    all_to_all x1 -> x0, waiting for transfers between devices: 43 us -> none  [to_cells(): lax.all_to_all(values, 'tracer', split_axis=1, concat_axis=0, tiled=True)]
    select_n x4 -> x0, other arithmetic: 28.3 us -> none  [face_flux(): return jnp.where(speed > 0.0, positive, negative)]
    ppermute x10 -> x0, starting transfers between devices: 18.9 us -> none  [the longest x5 13.7 us: padded(): lax.ppermute(lax.slice_in_dim(block, 0, width, axis=dim), axis, backward)]
    sub x2 -> x0, other arithmetic: 15.5 us -> none  [flux_substep(): return middle - sub_step * spread]
    dot_general x3 -> x0, matrix products: 12.8 us -> none  [the longest x1 4.54 us: optical_thickness(): jnp.tensordot(attenuation_factor, jnp.abs(by_cells), axes=1, precision=la...]
    slice x14 -> x0, local copies, waits for them, and re-layouts: 7.61 us -> none  [the longest x4 3.4 us: shift_south(): values[..., :-1]]
    all_gather x1 -> x0, blocking collectives: 5.24 us -> none  [prefix(): gathered = lax.all_gather(part, axis)]
  transfers between devices with their start and end apart: 11 -> 0, of which waited for: 3 -> 0; matrix products, arithmetic and copies ran while one was open for 45% -> 0% of each run, Pallas kernels for 0% -> 0%
where the time goes in v1:
time: 177 us
  Pallas kernels  170 us (96%)
  local copies, waits for them, and re-layouts  5.69 us (3%)
    pallas_call x1, Pallas kernels, on_device(): pl.pallas_call(functools.partial(transport_kernel, tiles, ranks, cores, q...  165 us
    unnamed x16, local copies, waits for them, and re-layouts  5.69 us
    pallas_call x1, Pallas kernels, on_device(): pl.pallas_call(functools.partial(react_kernel, nl, per), grid=(per,), out...  5.39 us

profile of v1, /device:TPU:0, one launch (start us, length us, event | category | flops | bytes accessed | tf_op | source)
XLA Modules:
  0.0 176.7 jit_solution(541383317133831912)
XLA Ops:
  0.6 0.0 copy-start
  0.6 2.2 %copy-done = f32[8,32,32,128]{3,2,1,0:T(8,128)S(1)} copy-done((f32[8,32,32,128]{3,2,1,0:T(8,128)S(1)}, f32[8,32,32,128]{3,2,1,0:T(8,128)}, u32[]{:S(2)}) %copy-start) | copy-done | bytes 4194328
  2.8 0.0 copy-start.1
  2.8 1.2 copy-done.1
  4.0 0.0 copy-start.2
  4.0 0.9 copy-done.2
  5.0 0.0 copy-start.3
  5.0 0.7 copy-done.3
  5.7 0.0 copy-start.5
  5.7 0.7 copy-done.5
  6.3 0.0 copy-start.4
  6.3 0.0 copy-start.6
  6.3 0.0 copy-start.7
  6.3 164.9 %transport.1 = (f32[32,8,32,128]{3,2,1,0:T(8,128)S(1)}, f32[4,32,128]{2,1,0:T(8,128)S(1)}, f32[2,8,32,128]{3,2,1,0:T(8,128)S(1)}, f32[8,32,128]{2,1,0:T(8,128)S(1)}) custom-call(f32[8,32,32,128]{3,2,1,0:T(8,128)S(1)} %copy-done, f32[2,32,32,128]{3,2,1,0:T(8,128)S(1)} %copy-done.1, f32[8,32,128]{2,1,0:T(8,128)S(1)} %copy-done.2, s32[32,128]{1,0:T(8,128)S(1)} %copy-done.3, ...), custom_call_target="tpu_custom_call" | custom-call | tf_op jit(solution)/shard_map/transport/pallas_call | solution.py:372
  171.3 0.0 copy-done.4
  171.3 0.0 copy-done.6
  171.3 0.0 copy-done.7
  171.3 5.4 %react.1 = (f32[32,8,32,128]{3,2,1,0:T(8,128)}, f32[2,8,32,128]{3,2,1,0:T(8,128)}, f32[8,32,128]{2,1,0:T(8,128)}) custom-call(f32[32,8,32,128]{3,2,1,0:T(8,128)S(1)} %get-tuple-element.7.cells, f32[4,32,128]{2,1,0:T(8,128)S(1)} %get-tuple-element.8.over, f32[2,8,32,128]{3,2,1,0:T(8,128)S(1)} %get-tuple-element.9.vel, ...), custom_call_target="tpu_custom_call" | custom-call | tf_op jit(solution)/shard_map/react/pallas_call | solution.py:410
Async XLA Ops:
  0.6 2.2 %copy-start = (f32[8,32,32,128]{3,2,1,0:T(8,128)S(1)}, f32[8,32,32,128]{3,2,1,0:T(8,128)}, u32[]{:S(2)}) copy-start(f32[8,32,32,128]{3,2,1,0:T(8,128)} %sp.1) | copy-start | bytes 12582916
  2.8 1.2 copy-start.1
  4.0 0.9 copy-start.2
  5.0 0.7 copy-start.3
  5.7 0.7 copy-start.5
  6.3 165.0 %copy-start.4 = (f32[32,128]{1,0:T(8,128)S(1)}, f32[32,128]{1,0:T(8,128)}, u32[]{:S(2)}) copy-start(f32[32,128]{1,0:T(8,128)} %sun.1) | copy-start | bytes 49156
  6.3 165.0 %copy-start.6 = (s32[32]{0:T(128)S(1)}, s32[32]{0:T(128)}, u32[]{:S(2)}) copy-start(s32[32]{0:T(128)} %eaten.1) | copy-start | bytes 388
  6.3 165.0 %copy-start.7 = (f32[32]{0:T(128)S(1)}, f32[32]{0:T(128)}, u32[]{:S(2)}) copy-start(f32[32]{0:T(128)} %rate.1) | copy-start | bytes 388

commit v2 on v1

--- a/solution.py
+++ b/solution.py
@@ -224,7 +224,7 @@
                 adv[t, lev] = c
                 return acc + att[r * nt + t] * jnp.abs(c)
 
-            tot[block] = lax.fori_loop(0, nt, one_tracer, tot[block])
+            tot[block] = lax.fori_loop(0, nt, one_tracer, tot[block], unroll=4)
             return carry
 
         lax.fori_loop(0, q, one_level, 0)
@@ -395,7 +395,7 @@
                 dma((chunks,)), dma((4,)), dma((1,)), dma((per // q,)),
             ],
             compiler_params=pltpu.CompilerParams(
-                collective_id=0, has_side_effects=True, vmem_limit_bytes=32 * 2**20
+                collective_id=0, has_side_effects=True
             ),
             name="transport",
         )(
@@ -427,7 +427,7 @@
                 pltpu.SMEM((count,), jnp.int32),
             ],
             compiler_params=pltpu.CompilerParams(
-                dimension_semantics=("arbitrary",), vmem_limit_bytes=16 * 2**20
+                dimension_semantics=("arbitrary",)
             ),
             name="react",
         )(

time: 177 us -> 70 us (0.40)
  Pallas kernels: 170 us -> 69.1 us
  local copies, waits for them, and re-layouts: 5.69 us -> 0 us
    pallas_call x1, Pallas kernels: 165 us -> 61.5 us  [on_device(): pl.pallas_call(functools.partial(transport_kernel, tiles, ranks, cores, q...]
    unnamed x16 -> x0, local copies, waits for them, and re-layouts: 5.69 us -> none
    pallas_call x1, Pallas kernels: 5.39 us -> 7.52 us  [on_device(): pl.pallas_call(functools.partial(react_kernel, nl, per), grid=(per,), out...]
where the time goes in v2:
time: 70 us; the launch traced here: 69.7 us
  Pallas kernels  69.1 us (99%)
    pallas_call x1, Pallas kernels, on_device(): pl.pallas_call(functools.partial(transport_kernel, tiles, ranks, cores, q...  61.5 us
    pallas_call x1, Pallas kernels, on_device(): pl.pallas_call(functools.partial(react_kernel, nl, per), grid=(per,), out...  7.52 us

profile of v2, /device:TPU:0, one launch (start us, length us, event | category | flops | bytes accessed | tf_op | source)
XLA Modules:
  0.0 69.7 jit_solution(13356912111690601418)
XLA Ops:
  0.6 61.5 %transport.1 = (f32[32,8,32,128]{3,2,1,0:T(8,128)}, f32[4,32,128]{2,1,0:T(8,128)}, f32[2,8,32,128]{3,2,1,0:T(8,128)}, f32[8,32,128]{2,1,0:T(8,128)}) custom-call(f32[8,32,32,128]{3,2,1,0:T(8,128)} %sp.1, f32[2,32,32,128]{3,2,1,0:T(8,128)} %fc.1, f32[8,32,128]{2,1,0:T(8,128)} %th.1, s32[32,128]{1,0:T(8,128)} %dep.3, f32[32]{0:T(128)} %att.3), custom_call_target="tpu_custom_call" | custom-call | tf_op jit(solution)/shard_map/transport/pallas_call | solution.py:372
  62.2 7.5 %react.1 = (f32[32,8,32,128]{3,2,1,0:T(8,128)}, f32[2,8,32,128]{3,2,1,0:T(8,128)}, f32[8,32,128]{2,1,0:T(8,128)}) custom-call(f32[32,8,32,128]{3,2,1,0:T(8,128)} %get-tuple-element.7.cells, f32[4,32,128]{2,1,0:T(8,128)} %get-tuple-element.8.over, f32[2,8,32,128]{3,2,1,0:T(8,128)} %get-tuple-element.9.vel, f32[8,32,128]{2,1,0:T(8,128)} %get-tuple-element.10.heat, ...), custom_call_target="tpu_custom_call" | custom-call | tf_op jit(solution)/shard_map/react/pallas_call | solution.py:410

commit v3 on v2

--- a/solution.py
+++ b/solution.py
@@ -224,7 +224,7 @@
                 adv[t, lev] = c
                 return acc + att[r * nt + t] * jnp.abs(c)
 
-            tot[block] = lax.fori_loop(0, nt, one_tracer, tot[block], unroll=4)
+            tot[block] = lax.fori_loop(0, nt, one_tracer, tot[block], unroll=True)
             return carry
 
         lax.fori_loop(0, q, one_level, 0)

time: 70 us -> 69.1 us (0.987)
  Pallas kernels: 69.1 us -> 68.2 us
    pallas_call x1, Pallas kernels: 61.5 us -> 60.7 us  [on_device(): pl.pallas_call(functools.partial(transport_kernel, tiles, ranks, cores, q...]
where the time goes in v3:
time: 69.1 us; the launch traced here: 68.8 us
  Pallas kernels  68.2 us (99%)
    pallas_call x1, Pallas kernels, on_device(): pl.pallas_call(functools.partial(transport_kernel, tiles, ranks, cores, q...  60.7 us
    pallas_call x1, Pallas kernels, on_device(): pl.pallas_call(functools.partial(react_kernel, nl, per), grid=(per,), out...  7.52 us

profile of v3, /device:TPU:0, one launch (start us, length us, event | category | flops | bytes accessed | tf_op | source)
XLA Modules:
  0.0 68.8 jit_solution(11621567003500228779)
XLA Ops:
  0.6 60.7 %transport.1 = (f32[32,8,32,128]{3,2,1,0:T(8,128)}, f32[4,32,128]{2,1,0:T(8,128)}, f32[2,8,32,128]{3,2,1,0:T(8,128)}, f32[8,32,128]{2,1,0:T(8,128)}) custom-call(f32[8,32,32,128]{3,2,1,0:T(8,128)} %sp.1, f32[2,32,32,128]{3,2,1,0:T(8,128)} %fc.1, f32[8,32,128]{2,1,0:T(8,128)} %th.1, s32[32,128]{1,0:T(8,128)} %dep.3, f32[32]{0:T(128)} %att.3), custom_call_target="tpu_custom_call" | custom-call | tf_op jit(solution)/shard_map/transport/pallas_call | solution.py:372
  61.3 7.5 %react.1 = (f32[32,8,32,128]{3,2,1,0:T(8,128)}, f32[2,8,32,128]{3,2,1,0:T(8,128)}, f32[8,32,128]{2,1,0:T(8,128)}) custom-call(f32[32,8,32,128]{3,2,1,0:T(8,128)} %get-tuple-element.7.cells, f32[4,32,128]{2,1,0:T(8,128)} %get-tuple-element.8.over, f32[2,8,32,128]{3,2,1,0:T(8,128)} %get-tuple-element.9.vel, f32[8,32,128]{2,1,0:T(8,128)} %get-tuple-element.10.heat, ...), custom_call_target="tpu_custom_call" | custom-call | tf_op jit(solution)/shard_map/react/pallas_call | solution.py:410
